TPU v7x, 512 devices: a whole 4x4x16 slice. The times are simulated.
512 devices in a mesh: ctx: 64 (over z, y_hi, core), req: 8 (over y_lo, x).
Axes of the slice: x: 4, y: 4 (y_hi: 2, y_lo: 2; y = y_hi * 2 + y_lo), z: 16, core: 2. Of those that a mesh axis runs over, the one named last changes fastest.
Arguments:
- hidden: bfloat16 [1024, 5120], P('req'), parts along dimension 0, may hold values from -6 to 6
- w_query: bfloat16 [5120, 8192], P(None, 'ctx'), may hold values from -0.078125 to 0.078125
- key_projection_weight: bfloat16 [5120, 1024], P(None, 'ctx'), may hold values from -0.078125 to 0.078125
- value_projection_weight: bfloat16 [5120, 1024], P(None, 'ctx'), may hold values from -0.078125 to 0.078125
- query_gain: float32 [128], replicated, may hold values from 0.5 to 1.5
- key_gain: float32 [128], replicated, may hold values from 4 to 8
- stored_cache_keys: bfloat16 [65536, 1024], P(('req', 'ctx')), parts along dimension 0, may hold values from -100 to 100
- stored_cache_values: bfloat16 [65536, 1024], P(('req', 'ctx')), parts along dimension 0, may hold values from -8 to 8
- cache_length: int32 [8], P('req'), parts along dimension 0, may hold values from 4096 to 8192
- first_position: int32 [8], P('req'), parts along dimension 0, may hold values from 0 to 4095
Outputs:
- attended: bfloat16 [1024, 8192], P('req', 'ctx'), parts along dimension 0
There are 8 independent parts, one for each index of `req`. A program takes and returns all parts, laid end to end along the dimension named above; an argument that names none is the same for every part. Nothing has to cross between parts.
All inputs are finite; a program needn't handle non-finite values.
Results may differ from a plain program's by a relative error of at most 0.013.
The roundings to bfloat16 on the way count: a program that leaves them out, or rounds other values in their place, can miss the bound.
Values may be sent and summed in bfloat16 or wider, within the bound.
No kernel may reach another device: no remote copies, remote signals or barrier semaphores. Data moves between devices by JAX's collectives and lax.ppermute only.
A program may use at most 128 MiB of HBM per device.

v0:
```python
import math
import jax
import jax.numpy as jnp
from jax import lax
from jax.sharding import Mesh
from jax.sharding import PartitionSpec as P

CTX = ("ctx_0", "ctx_1", "ctx_2")
REQ_CTX = ("req", "ctx_0", "ctx_1", "ctx_2")


def gather_turned(arrays, axis, dims):
    turned = [jnp.moveaxis(a, dim, 0) for a, dim in zip(arrays, dims)]
    widths = [t[0].size for t in turned]
    both = jnp.concatenate([t.reshape(-1, w) for t, w in zip(turned, widths)], axis=1)
    filled = lax.all_gather(both, axis, axis=0, tiled=True)
    pieces = jnp.split(filled, [sum(widths[:k]) for k in range(1, len(widths))], axis=1)
    return tuple(
        (
            jnp.moveaxis(b.reshape(-1, *t.shape[1:]), 0, dim)
            for b, t, dim in zip(pieces, turned, dims)
        )
    )


def laid_out(pieces, dim):
    shape = list(pieces.shape[1:])
    shape[dim] *= pieces.shape[0]
    return jnp.moveaxis(pieces, 0, dim).reshape(shape)


def gather_in_order(value, axes, turns):
    pieces = value
    for k in turns:
        pieces = lax.all_gather(pieces, axes[k])
    done = turns[::-1]
    back = [done.index(k) for k in range(len(axes))]
    pieces = pieces.transpose(*back, *range(len(axes), pieces.ndim))
    return pieces.reshape(-1, *value.shape)


def gather_axes(value, axes, turns, dim):
    return laid_out(gather_in_order(value, axes, turns), dim)


def sent_together(arrays, axis, split_dim, concat_dim, along):
    columns = [a.reshape(*a.shape[:along], -1) for a in arrays]
    both = jnp.concatenate(columns, axis=along)
    filled, at, outs = (
        lax.all_to_all(both, axis, split_axis=split_dim, concat_axis=concat_dim, tiled=True),
        0,
        [],
    )
    for a, column in zip(arrays, columns):
        section = filled[..., at : at + column.shape[along]]
        outs.append(section.reshape(*section.shape[:along], *a.shape[along:]))
        at += column.shape[along]
    return tuple(outs)


def normalize(joined_values, gain):
    mean_square = jnp.mean(joined_values * joined_values, axis=-1, keepdims=True)
    return joined_values * lax.rsqrt(mean_square + 1e-06) * gain


def rotate(joined_values, positions):
    half = joined_values.shape[-1] // 2
    freq = jnp.exp(
        jnp.arange(half, dtype=jnp.float32) * (-2.0 * math.log(1000000.0) / joined_values.shape[-1])
    )
    angles = positions[:, None] * freq[None, :]
    cosine = jnp.concatenate([jnp.cos(angles), jnp.cos(angles)], axis=-1)[:, None, :]
    sine = jnp.concatenate([jnp.sin(angles), jnp.sin(angles)], axis=-1)[:, None, :]
    turned = jnp.concatenate([-joined_values[..., half:], joined_values[..., :half]], axis=-1)
    return joined_values * cosine + turned * sine


def soft_weights(scores, visible):
    masked = jnp.where(visible, scores, -1e30)
    top = jnp.max(masked, axis=-1)
    weights = jnp.where(visible, jnp.exp(masked - top[..., None]), 0.0)
    return (weights, top, jnp.sum(weights, axis=-1))


def join(first, second):
    top = jnp.maximum(first[1], second[1])
    scale_a = jnp.exp(first[1] - top)
    scale_b = jnp.exp(second[1] - top)
    summed = first[0] * scale_a[..., None] + second[0] * scale_b[..., None]
    return (summed, top, first[2] * scale_a + second[2] * scale_b)


def fold_sources(received):
    sums, maxima, totals = received
    top = jnp.max(maxima, axis=1)
    factor = jnp.exp(maxima - top[:, None])
    return (jnp.sum(sums * factor[..., None], axis=1), top, jnp.sum(totals * factor, axis=1))


def per_device(
    hidden,
    w_query,
    key_projection_weight,
    value_projection_weight,
    query_gain,
    key_gain,
    stored_cache_keys,
    stored_cache_values,
    cache_length,
    first_position,
):
    groups = lax.axis_size(CTX)
    rank = lax.axis_index(CTX)
    input_tokens = hidden.shape[0]
    head_dim = query_gain.shape[0]
    heads_here = w_query.shape[1] // head_dim
    all_heads = heads_here * groups
    kv_heads = stored_cache_keys.shape[1] // head_dim
    query_group = all_heads // kv_heads
    slots = stored_cache_keys.shape[0]
    scale = 1.0 / math.sqrt(head_dim)
    positions = first_position[0].astype(jnp.float32) + jnp.arange(input_tokens, dtype=jnp.float32)
    projected = jnp.dot(hidden, w_query, preferred_element_type=jnp.float32).reshape(
        input_tokens, heads_here, head_dim
    )
    own_queries = (
        rotate(normalize(projected, query_gain), positions).astype(jnp.bfloat16).transpose(1, 0, 2)
    )
    key_part = jnp.dot(hidden, key_projection_weight, preferred_element_type=jnp.float32).astype(
        jnp.bfloat16
    )
    value_part = jnp.dot(
        hidden, value_projection_weight, preferred_element_type=jnp.float32
    ).astype(jnp.bfloat16)
    key_full, value_full = gather_turned((key_part, value_part), CTX, (1, 1))
    key_float = (
        key_full.astype(jnp.float32).reshape(input_tokens, head_dim, kv_heads).transpose(0, 2, 1)
    )
    incoming_keys = rotate(normalize(key_float, key_gain), positions).astype(jnp.bfloat16)
    incoming_values = value_full.reshape(input_tokens, head_dim, kv_heads).transpose(0, 2, 1)
    query_states = gather_axes(own_queries, CTX, (1, 0, 2), 0)
    token_rows = query_states.reshape(kv_heads, query_group * input_tokens, head_dim)
    valid = (rank * slots + jnp.arange(slots, dtype=jnp.int32) < cache_length[0])[None, :]

    def shard_term(index):
        query_rows = lax.dynamic_index_in_dim(token_rows, index, 0, keepdims=False)
        key_rows = lax.dynamic_slice_in_dim(stored_cache_keys, index * head_dim, head_dim, 1)
        value_rows = lax.dynamic_slice_in_dim(stored_cache_values, index * head_dim, head_dim, 1)
        scores = (
            lax.dot_general(
                query_rows, key_rows, (((1,), (1,)), ((), ())), preferred_element_type=jnp.float32
            )
            * scale
        )
        weights, top, total = soft_weights(scores, valid)
        summed = jnp.dot(
            weights.astype(jnp.bfloat16), value_rows, preferred_element_type=jnp.float32
        )
        return (summed, top, total)

    sums, maxima, totals = lax.map(shard_term, jnp.arange(kv_heads, dtype=jnp.int32))
    sums = sums.reshape(all_heads, input_tokens, head_dim)
    maxima = maxima.reshape(all_heads, input_tokens)
    totals = totals.reshape(all_heads, input_tokens)
    received = sent_together((sums[:, None], maxima[:, None], totals[:, None]), CTX, 0, 1, 3)
    merged = fold_sources(received)
    head_ids = rank * heads_here + jnp.arange(heads_here, dtype=jnp.int32)
    chosen = head_ids // query_group
    keys_here = jnp.take(incoming_keys, chosen, axis=1)
    values_here = jnp.take(incoming_values, chosen, axis=1)
    scores = (
        jnp.einsum("htd,shd->hts", own_queries, keys_here, preferred_element_type=jnp.float32)
        * scale
    )
    causal = (jnp.arange(input_tokens)[None, :] <= jnp.arange(input_tokens)[:, None])[None]
    weights, top, total = soft_weights(scores, causal)
    fresh = jnp.einsum(
        "hts,shd->htd",
        weights.astype(jnp.bfloat16),
        values_here,
        preferred_element_type=jnp.float32,
    )
    final = join((fresh, top, total), merged)
    attention_output = final[0] / final[2][..., None]
    return (
        attention_output.transpose(1, 0, 2)
        .reshape(input_tokens, heads_here * head_dim)
        .astype(jnp.bfloat16)
    )


def solution(mesh):
    finer = Mesh(
        mesh.devices.reshape(16, 2, 2, mesh.shape["req"]), ("ctx_0", "ctx_1", "ctx_2", "req")
    )
    return jax.shard_map(
        per_device,
        mesh=finer,
        in_specs=(
            P("req", None),
            P(None, CTX),
            P(None, CTX),
            P(None, CTX),
            P(),
            P(),
            P(REQ_CTX, None),
            P(REQ_CTX, None),
            P("req"),
            P("req"),
        ),
        out_specs=P("req", CTX),
        check_vma=False,
    )
```

profile of v0, /device:TPU:1, one launch (start us, length us, event | category | flops | bytes accessed | tf_op | source)
XLA Modules:
  0.0 499.5 jit_solution(5183464044391376757)
XLA Ops:
  6.5 1.3 copy-done
  7.9 2.0 multiply_reduce_fusion.1
  9.8 0.7 fusion.28
  11.4 1.3 pad_maximum_fusion.1
  12.7 5.7 %all-gather = bf16[256,128]{0,1:T(8,128)(2,1)S(1)} all-gather(bf16[128,128]{0,1:T(8,128)(2,1)S(1)} %get-tuple-element.125), channel_id=2, replica_groups=mesh['ctx_0'=16,'ctx_1'=2,'ctx_2'=2,'req'=8] {'ctx_1'}, dimensions={0}, use_global_device_ids=true | all-gather | bytes 98304 | tf_op jit(solution)/shard_map/all_gather | solution.py:35
  18.5 0.7 copy.70
  19.2 66.1 %all-gather.6.cloned.1.call-done = bf16[32,1,128,128]{3,2,1,0:T(8,128)(2,1)} async-done(((bf16[2,1,128,128]{3,2,1,0:T(8,128)(2,1)}), bf16[32,1,128,128]{3,2,1,0:T(8,128)(2,1)}) %all-gather.6.cloned.1.call-update) | async-done | bytes 1048592 | tf_op jit(solution)/shard_map/all_gather | solution.py:35
  85.4 31.9 %all-gather.8.cloned.1.call-done = bf16[32,2,1,128,128]{4,3,2,1,0:T(8,128)(2,1)} async-done(((bf16[16,2,1,128,128]{4,3,2,1,0:T(8,128)(2,1)}), bf16[32,2,1,128,128]{4,3,2,1,0:T(8,128)(2,1)}) %all-gather.8.cloned.1.call-update) | async-done | bytes 2097168 | tf_op jit(solution)/shard_map/all_gather | solution.py:35
  117.3 1.7 copy.64
  119.1 69.1 %while.16 = (s32[]{:T(128)}, f32[8,1024,128]{2,1,0:T(8,128)}, f32[8,1024]{1,0:T(8,128)S(1)}, f32[8,1024]{1,0:T(8,128)}, s32[8]{0:T(128)S(1)}, /*index=5*/bf16[8,...) while((s32[]{:T(128)}, f32[8,1024,128]{2,1,0:T(8,128)}, ...), condition=%wide.region_6.8_spmd.clone, body=%wide.region_3.7_spmd.clone.sunk | while | flops 68286728 | bytes 2459269 | solution.py:161
  119.1 0.7 dynamic_slice.37
  123.2 1.0 fusion.75
  124.2 1.9 fusion.76
  126.2 1.4 dynamic_update_slice.20
  127.7 0.7 dynamic_slice.37
  131.8 1.0 fusion.75
  132.8 2.0 fusion.76
  134.9 1.4 dynamic_update_slice.20
  140.5 1.0 fusion.75
  141.5 1.9 fusion.76
  143.6 1.4 dynamic_update_slice.20
  145.0 0.7 dynamic_slice.37
  149.1 1.0 fusion.75
  150.2 1.9 fusion.76
  152.2 1.4 dynamic_update_slice.20
  157.7 1.0 fusion.75
  158.8 1.9 fusion.76
  160.8 1.4 dynamic_update_slice.20
  162.3 0.7 dynamic_slice.37
  166.4 1.0 fusion.75
  167.4 1.9 fusion.76
  169.4 1.4 dynamic_update_slice.20
  170.9 0.7 dynamic_slice.37
  175.0 1.0 fusion.75
  176.0 1.9 fusion.76
  178.1 1.4 dynamic_update_slice.20
  183.6 1.0 fusion.75
  184.7 1.9 fusion.76
  186.7 1.4 dynamic_update_slice.20
  188.2 6.0 %reshape_broadcast_in_dim_reshape.8 = f32[64,1,128,1]{3,2,0,1:T(8,128)} reshape(f32[8,1024]{1,0:T(8,128)S(1)} %get-tuple-element.56) | data formatting | bytes 65536 | tf_op jit(solution)/shard_map/reshape;broadcast_in_dim;reshape | solution.py:47
  194.2 6.1 %reshape_broadcast_in_dim_reshape.9 = f32[64,1,128,1]{3,2,0,1:T(8,128)} reshape(f32[8,1024]{1,0:T(8,128)S(1)} %copy-done.4) | data formatting | bytes 65536 | tf_op jit(solution)/shard_map/reshape;broadcast_in_dim;reshape | solution.py:47
  200.3 7.6 %pad_maximum_fusion = f32[64,1,128,130]{3,2,0,1:T(8,128)} fusion(f32[64,1,128,1]{3,2,0,1:T(8,128)} %reshape_broadcast_in_dim_reshape.9, f32[64,1,128,1]{3,2,0,1:T(8,128)} %reshape_broadcast_in_dim_reshape.8, f32[64,1,128,128]{3,2,0,1:T(8,128)} %bitcast.98), kind=kLoop, calls=%fused_computation.19 | loop fusion | flops 2129920 | bytes 8519680 | tf_op jit(solution)/shard_map/concatenate | solution.py:48
  207.9 12.4 %copy.67 = f32[64,1,128,130]{2,1,3,0:T(1,128)} copy(f32[64,1,128,130]{3,2,0,1:T(8,128)} %pad_maximum_fusion) | data formatting | bytes 8519680 | tf_op jit(solution)/shard_map/concatenate | solution.py:48
  220.2 14.7 %all-to-all-start = ((f32[64,1,128,130]{2,1,3,0:T(1,128)}), f32[64,1,128,130]{2,1,3,0:T(1,128)}, u32[]{:S(2)}, u32[]{:S(2)}) async-start(f32[64,1,128,130]{2,1,3,0:T(1,128)} %copy.67), calls=%async_computation | async-start | bytes 8519680 | tf_op jit(solution)/shard_map/all_to_all | solution.py:50
  236.1 250.6 %all_gather.18 = bf16[1024,256]{1,0:T(8,128)(2,1)S(1)} all-gather(bf16[16,256]{1,0:T(8,128)(2,1)S(1)} %pad_maximum_fusion.3), channel_id=1, replica_groups=mesh['ctx_0'=16,'ctx_1'=2,'ctx_2'=2,'req'=8] {'ctx_0','ctx_1','ctx_2'}, dimensions={0}, use_global_device_ids=true | all-gather | bytes 532480 | tf_op jit(solution)/shard_map/all_gather | solution.py:16
  488.1 2.8 copy.72
  491.0 0.7 fusion.17
  491.9 0.8 fusion.21
  (71 shorter events, 11.7 us)
Async XLA Ops:
  6.5 1.3 copy-start
  6.5 78.8 %all-gather.6.cloned.1.call-start = ((), (), s32[]{:S(2)}) async-start(), calls=%async_computation.1 | async-start | bytes 1114112 | tf_op jit(solution)/shard_map/all_gather | solution.py:35
  19.2 98.1 %all-gather.8.cloned.1.call-start = ((), (), s32[]{:S(2)}) async-start(), calls=%async_computation.2 | async-start | bytes 3145728 | tf_op jit(solution)/shard_map/all_gather | solution.py:35
  188.2 6.1 %copy-start.4 = (f32[8,1024]{1,0:T(8,128)S(1)}, f32[8,1024]{1,0:T(8,128)}, u32[]{:S(2)}) copy-start(f32[8,1024]{1,0:T(8,128)} %get-tuple-element.57) | copy-start | bytes 98308
  220.2 14.8 %copy-start.1 = (f32[128,128]{0,1:T(8,128)S(1)}, f32[128,128]{0,1:T(8,128)}, u32[]{:S(2)}) copy-start(f32[128,128]{0,1:T(8,128)} %get-tuple-element.124) | copy-start | bytes 196612
  220.2 15.0 %copy-start.2 = (bf16[5120,16]{0,1:T(8,128)(2,1)S(1)}, bf16[5120,16]{0,1:T(8,128)(2,1)}, u32[]{:S(2)}) copy-start(bf16[5120,16]{0,1:T(8,128)(2,1)} %param.17) | copy-start | bytes 491524
  220.2 15.4 %copy-start.3 = (bf16[5120,16]{0,1:T(8,128)(2,1)S(1)}, bf16[5120,16]{0,1:T(8,128)(2,1)}, u32[]{:S(2)}) copy-start(bf16[5120,16]{0,1:T(8,128)(2,1)} %param.16) | copy-start | bytes 491524
  220.2 267.9 %all-to-all-start = ((f32[64,1,128,130]{2,1,3,0:T(1,128)}), f32[64,1,128,130]{2,1,3,0:T(1,128)}, u32[]{:S(2)}, u32[]{:S(2)}) async-start(f32[64,1,128,130]{2,1,3,0:T(1,128)} %copy.67), calls=%async_computation | async-start | bytes 8519680 | tf_op jit(solution)/shard_map/all_to_all | solution.py:50
  235.0 252.5 %copy-start.5 = (f32[128]{0:T(128)S(1)}, f32[128]{0:T(128)}, u32[]{:S(2)}) copy-start(f32[128]{0:T(128)} %param.19) | copy-start | bytes 1540
Sparse Core Ops, SparseCore 0:
  19.3 66.0 all-gather.5
  87.5 29.8 all-gather.7
where the time goes:
time: 502 us; the launch traced here: 500 us
  blocking collectives  256 us (51%)
  waiting for transfers between devices  98 us (20%)
  local copies, waits for them, and re-layouts  48.9 us (10%)
  matrix products  27.3 us (5%)
  loops' own time  22.5 us (4%)
  other arithmetic  17.5 us (3%)
  starting transfers between devices  14.8 us (3%)
  between operations  14.3 us (3%)
    all_gather x1, blocking collectives, gather_turned(): filled = lax.all_gather(both, axis, axis=0, tiled=True)  251 us
    all_gather x2, waiting for transfers between devices, gather_in_order(): pieces = lax.all_gather(pieces, axes[k])  98 us
    another operation x1, loops' own time, per_device(): lax.map(shard_term, jnp.arange(kv_heads, dtype=jnp.int32))  22.5 us
    dot_general x8, matrix products, shard_term(): jnp.dot(weights.astype(jnp.bfloat16), value_rows, preferred_element_type=...  15.3 us
    all_to_all x1, starting transfers between devices, sent_together(): lax.all_to_all(both, axis, split_axis=split_dim, concat_axis=concat_dim,...  14.7 us
    concatenate x1, local copies, waits for them, and re-layouts, sent_together(): both = jnp.concatenate(columns, axis=along)  12.4 us
    another operation x2, local copies, waits for them, and re-layouts, sent_together(): columns = [a.reshape(*a.shape[:along], -1) for a in arrays]  12.1 us
    dynamic_update_slice x16, local copies, waits for them, and re-layouts, per_device(): lax.map(shard_term, jnp.arange(kv_heads, dtype=jnp.int32))  11.7 us
  transfers between devices with their start and end apart: 3, of which 2 were waited for; matrix products, arithmetic and copies ran while one was open for 0% of the time, Pallas kernels for 0%

commit v1 on v0

--- a/solution.py
+++ b/solution.py
@@ -9,11 +9,16 @@
 REQ_CTX = ("req", "ctx_0", "ctx_1", "ctx_2")
 
 
+def gather_over(array, name, dim):
+    outgoing = jnp.stack([array] * lax.axis_size(name))
+    return jnp.concatenate(lax.all_to_all(outgoing, name, 0, 0), axis=dim)
+
+
 def gather_turned(arrays, axis, dims):
     turned = [jnp.moveaxis(a, dim, 0) for a, dim in zip(arrays, dims)]
     widths = [t[0].size for t in turned]
     both = jnp.concatenate([t.reshape(-1, w) for t, w in zip(turned, widths)], axis=1)
-    filled = lax.all_gather(both, axis, axis=0, tiled=True)
+    filled = gather_over(both, axis, 0)
     pieces = jnp.split(filled, [sum(widths[:k]) for k in range(1, len(widths))], axis=1)
     return tuple(
         (

time: 502 us -> 442 us (0.88)
  blocking collectives: 256 us -> 5.71 us
  waiting for transfers between devices: 98 us -> 259 us
  starting transfers between devices: 14.8 us -> 36.8 us
    all_gather x1 -> x0, blocking collectives: 251 us -> none  [gather_turned(): filled = lax.all_gather(both, axis, axis=0, tiled=True)]
    all_to_all x1, waiting for transfers between devices: 0.01 us -> 185 us  [sent_together(): lax.all_to_all(both, axis, split_axis=split_dim, concat_axis=concat_dim,...]
    all_gather x2, waiting for transfers between devices: 98 us -> 74.2 us  [gather_in_order(): pieces = lax.all_gather(pieces, axes[k])]
    all_to_all x0 -> x1, starting transfers between devices: none -> 22 us  [gather_over(): return jnp.concatenate(lax.all_to_all(outgoing, name, 0, 0), axis=dim)]
  transfers between devices with their start and end apart: 3 -> 4, of which waited for: 2 -> 3; matrix products, arithmetic and copies ran while one was open for 0% -> 20% of each run, Pallas kernels for 0% -> 0%
where the time goes in v1:
time: 442 us; the launch traced here: 435 us
  waiting for transfers between devices  259 us (59%)
  local copies, waits for them, and re-layouts  50.4 us (11%)
  starting transfers between devices  36.8 us (8%)
  matrix products  27.2 us (6%)
  loops' own time  22.5 us (5%)
  other arithmetic  19.3 us (4%)
  between operations  14.3 us (3%)
  blocking collectives  5.71 us (1%)
    all_to_all x1, waiting for transfers between devices, sent_together(): lax.all_to_all(both, axis, split_axis=split_dim, concat_axis=concat_dim,...  185 us
    all_gather x2, waiting for transfers between devices, gather_in_order(): pieces = lax.all_gather(pieces, axes[k])  74.2 us
    another operation x1, loops' own time, per_device(): lax.map(shard_term, jnp.arange(kv_heads, dtype=jnp.int32))  22.5 us
    all_to_all x1, starting transfers between devices, gather_over(): return jnp.concatenate(lax.all_to_all(outgoing, name, 0, 0), axis=dim)  22 us
    dot_general x8, matrix products, shard_term(): jnp.dot(weights.astype(jnp.bfloat16), value_rows, preferred_element_type=...  15.4 us
    all_to_all x1, starting transfers between devices, sent_together(): lax.all_to_all(both, axis, split_axis=split_dim, concat_axis=concat_dim,...  14.7 us
    concatenate x1, local copies, waits for them, and re-layouts, sent_together(): both = jnp.concatenate(columns, axis=along)  12.4 us
    another operation x2, local copies, waits for them, and re-layouts, sent_together(): columns = [a.reshape(*a.shape[:along], -1) for a in arrays]  12.1 us
  transfers between devices with their start and end apart: 4, of which 3 were waited for; matrix products, arithmetic and copies ran while one was open for 20% of the time, Pallas kernels for 0%

profile of v1, /device:TPU:1, one launch (start us, length us, event | category | flops | bytes accessed | tf_op | source)
XLA Modules:
  0.0 435.2 jit_solution(3566522910754847145)
XLA Ops:
  6.6 1.3 copy-done
  7.9 2.0 multiply_reduce_fusion
  9.8 0.7 fusion.29
  11.4 1.3 pad_maximum_fusion.1
  12.7 5.7 %all-gather = bf16[256,128]{0,1:T(8,128)(2,1)S(1)} all-gather(bf16[128,128]{0,1:T(8,128)(2,1)S(1)} %get-tuple-element.123), channel_id=2, replica_groups=mesh['ctx_0'=16,'ctx_1'=2,'ctx_2'=2,'req'=8] {'ctx_1'}, dimensions={0}, use_global_device_ids=true | all-gather | bytes 98304 | tf_op jit(solution)/shard_map/all_gather | solution.py:40
  18.4 0.7 copy.60
  19.2 66.1 %all-gather.6.cloned.1.call-done = bf16[32,1,128,128]{3,2,1,0:T(8,128)(2,1)} async-done(((bf16[2,1,128,128]{3,2,1,0:T(8,128)(2,1)}), bf16[32,1,128,128]{3,2,1,0:T(8,128)(2,1)}) %all-gather.6.cloned.1.call-update) | async-done | bytes 1048592 | tf_op jit(solution)/shard_map/all_gather | solution.py:40
  86.3 0.9 stack.2
  87.2 22.0 %all-to-all-start = ((bf16[64,16,256]{2,1,0:T(8,128)(2,1)}), bf16[64,16,256]{2,1,0:T(8,128)(2,1)}, u32[]{:S(2)}, u32[]{:S(2)}) async-start(bf16[64,16,256]{2,1,0:T(8,128)(2,1)} %stack.2), calls=%async_computation | async-start | bytes 1048576 | tf_op jit(solution)/shard_map/all_to_all | solution.py:14
  109.3 8.0 %all-gather.8.cloned.1.call-done = bf16[32,2,1,128,128]{4,3,2,1,0:T(8,128)(2,1)} async-done(((bf16[16,2,1,128,128]{4,3,2,1,0:T(8,128)(2,1)}), bf16[32,2,1,128,128]{4,3,2,1,0:T(8,128)(2,1)}) %all-gather.8.cloned.1.call-update) | async-done | bytes 2097168 | tf_op jit(solution)/shard_map/all_gather | solution.py:40
  117.3 1.7 copy.54
  119.1 69.1 %while.16 = (s32[]{:T(128)}, f32[8,1024,128]{2,1,0:T(8,128)}, f32[8,1024]{1,0:T(8,128)S(1)}, f32[8,1024]{1,0:T(8,128)}, s32[8]{0:T(128)S(1)}, /*index=5*/bf16[8,...) while((s32[]{:T(128)}, f32[8,1024,128]{2,1,0:T(8,128)}, ...), condition=%wide.region_6.8_spmd.clone, body=%wide.region_3.7_spmd.clone.sunk | while | flops 68286728 | bytes 2459269 | solution.py:166
  123.2 1.0 fusion.68
  124.2 1.9 fusion.69
  126.2 1.4 dynamic_update_slice.20
  131.8 1.0 fusion.68
  132.8 2.0 fusion.69
  134.9 1.4 dynamic_update_slice.20
  140.5 1.0 fusion.68
  141.5 1.9 fusion.69
  143.5 1.4 dynamic_update_slice.20
  149.1 1.0 fusion.68
  150.1 1.9 fusion.69
  152.2 1.4 dynamic_update_slice.20
  157.7 1.0 fusion.68
  158.8 1.9 fusion.69
  160.8 1.4 dynamic_update_slice.20
  166.4 1.0 fusion.68
  167.4 1.9 fusion.69
  169.4 1.4 dynamic_update_slice.20
  175.0 1.0 fusion.68
  176.1 1.9 fusion.69
  178.1 1.4 dynamic_update_slice.20
  183.7 1.0 fusion.68
  184.7 1.9 fusion.69
  186.7 1.4 dynamic_update_slice.20
  188.2 6.0 %reshape_broadcast_in_dim_reshape.8 = f32[64,1,128,1]{3,2,0,1:T(8,128)} reshape(f32[8,1024]{1,0:T(8,128)S(1)} %get-tuple-element.56) | data formatting | bytes 65536 | tf_op jit(solution)/shard_map/reshape;broadcast_in_dim;reshape | solution.py:52
  194.2 6.1 %reshape_broadcast_in_dim_reshape.9 = f32[64,1,128,1]{3,2,0,1:T(8,128)} reshape(f32[8,1024]{1,0:T(8,128)S(1)} %copy-done.4) | data formatting | bytes 65536 | tf_op jit(solution)/shard_map/reshape;broadcast_in_dim;reshape | solution.py:52
  200.3 7.6 %pad_maximum_fusion = f32[64,1,128,130]{3,2,0,1:T(8,128)} fusion(f32[64,1,128,1]{3,2,0,1:T(8,128)} %reshape_broadcast_in_dim_reshape.9, f32[64,1,128,1]{3,2,0,1:T(8,128)} %reshape_broadcast_in_dim_reshape.8, f32[64,1,128,128]{3,2,0,1:T(8,128)} %bitcast.104), kind=kLoop, calls=%fused_computation.19 | loop fusion | flops 2129920 | bytes 8519680 | tf_op jit(solution)/shard_map/concatenate | solution.py:53
  207.9 12.4 %copy.57 = f32[64,1,128,130]{2,1,3,0:T(1,128)} copy(f32[64,1,128,130]{3,2,0,1:T(8,128)} %pad_maximum_fusion) | data formatting | bytes 8519680 | tf_op jit(solution)/shard_map/concatenate | solution.py:53
  220.3 14.7 %all-to-all-start.1 = ((f32[64,1,128,130]{2,1,3,0:T(1,128)}), f32[64,1,128,130]{2,1,3,0:T(1,128)}, u32[]{:S(2)}, u32[]{:S(2)}) async-start(f32[64,1,128,130]{2,1,3,0:T(1,128)} %copy.57), calls=%async_computation.1 | async-start | bytes 8519680 | tf_op jit(solution)/shard_map/all_to_all | solution.py:55
  235.0 1.1 fusion.22
  236.1 1.1 fusion.24
  237.6 1.0 slice_bitcast_fusion
  239.0 184.8 %all-to-all-done.1 = f32[64,1,128,130]{2,1,3,0:T(1,128)} async-done(((f32[64,1,128,130]{2,1,3,0:T(1,128)}), f32[64,1,128,130]{2,1,3,0:T(1,128)}, u32[]{:S(2)}, u32[]{:S(2)}) %all-to-all-start.1) | async-done | bytes 4259872 | tf_op jit(solution)/shard_map/all_to_all | solution.py:55
  423.8 2.8 copy.62
  426.7 0.7 fusion.17
  427.6 0.8 fusion.21
  (72 shorter events, 14.2 us)
Async XLA Ops:
  6.5 1.3 copy-start
  6.5 78.9 %copy-start.2 = (bf16[5120,16]{0,1:T(8,128)(2,1)S(1)}, bf16[5120,16]{0,1:T(8,128)(2,1)}, u32[]{:S(2)}) copy-start(bf16[5120,16]{0,1:T(8,128)(2,1)} %param.17) | copy-start | bytes 491524
  6.5 79.3 %copy-start.3 = (bf16[5120,16]{0,1:T(8,128)(2,1)S(1)}, bf16[5120,16]{0,1:T(8,128)(2,1)}, u32[]{:S(2)}) copy-start(bf16[5120,16]{0,1:T(8,128)(2,1)} %param.16) | copy-start | bytes 491524
  6.5 78.8 %all-gather.6.cloned.1.call-start = ((), (), s32[]{:S(2)}) async-start(), calls=%async_computation.2 | async-start | bytes 1114112 | tf_op jit(solution)/shard_map/all_gather | solution.py:40
  19.2 98.1 %all-gather.8.cloned.1.call-start = ((), (), s32[]{:S(2)}) async-start(), calls=%async_computation.3 | async-start | bytes 3145728 | tf_op jit(solution)/shard_map/all_gather | solution.py:40
  87.2 133.1 %all-to-all-start = ((bf16[64,16,256]{2,1,0:T(8,128)(2,1)}), bf16[64,16,256]{2,1,0:T(8,128)(2,1)}, u32[]{:S(2)}, u32[]{:S(2)}) async-start(bf16[64,16,256]{2,1,0:T(8,128)(2,1)} %stack.2), calls=%async_computation | async-start | bytes 1048576 | tf_op jit(solution)/shard_map/all_to_all | solution.py:14
  188.2 6.1 %copy-start.4 = (f32[8,1024]{1,0:T(8,128)S(1)}, f32[8,1024]{1,0:T(8,128)}, u32[]{:S(2)}) copy-start(f32[8,1024]{1,0:T(8,128)} %get-tuple-element.57) | copy-start | bytes 98308
  220.2 15.9 %copy-start.5 = (f32[128]{0:T(128)S(1)}, f32[128]{0:T(128)}, u32[]{:S(2)}) copy-start(f32[128]{0:T(128)} %param.19) | copy-start | bytes 1540
  220.2 17.1 %copy-start.1 = (f32[128,128]{0,1:T(8,128)S(1)}, f32[128,128]{0,1:T(8,128)}, u32[]{:S(2)}) copy-start(f32[128,128]{0,1:T(8,128)} %get-tuple-element.124) | copy-start | bytes 196612
  220.3 203.6 %all-to-all-start.1 = ((f32[64,1,128,130]{2,1,3,0:T(1,128)}), f32[64,1,128,130]{2,1,3,0:T(1,128)}, u32[]{:S(2)}, u32[]{:S(2)}) async-start(f32[64,1,128,130]{2,1,3,0:T(1,128)} %copy.57), calls=%async_computation.1 | async-start | bytes 8519680 | tf_op jit(solution)/shard_map/all_to_all | solution.py:55
Sparse Core Ops, SparseCore 0:
  19.3 66.0 all-gather.5
  87.5 29.8 all-gather.7
